TPU v7x, 8 devices: a whole 2x2x1 slice. The times are simulated.
8 devices in a mesh: sys: 1 (over z), aux: 2 (over y), orb: 4 (over x, core).
Axes of the slice: x: 2, y: 2, z: 1, core: 2. Of those that a mesh axis runs over, the one named last changes fastest.
Arguments:
- aux_ints: float32 [672, 192, 192], P(('sys', 'aux'), 'orb')
- metric: float32 [672, 672], P(('sys', 'aux'))
- orbitals: float32 [4, 192, 40], P('sys')
Outputs:
- output: float32 [4, 192, 192], P('sys', 'orb', 'aux')
All inputs are finite; a program needn't handle non-finite values.
Results may differ from a plain program's by a relative error of at most 0.001.
Values are sent between devices in bfloat16 or wider.
A program may use at most 1 GiB of HBM per device.

v0:
```python
import functools

import jax
import jax.numpy as jnp
from jax import lax
from jax.experimental import pallas as pl
from jax.experimental.pallas import tpu as pltpu
from jax.sharding import PartitionSpec as P

MESH = pl.DeviceIdType.MESH
F32, BF16 = jnp.float32, jnp.bfloat16
HIGHEST = lax.Precision.HIGHEST

DENS, L, OCC = 4, 192, 40
COLS = DENS * OCC
MINE = COLS // 8
ROWS = 48
GROUP = 16
GROUPS = ROWS // GROUP
QL, QP = 336, 384
TAIL = QL - 256
STRIDE = 168
HALFC = COLS // 2
MQ = 88
WPAD = 32
NT = (((1,), (1,)), ((), ()))


def _subsets(sizes):
    out, first, off = [], 0, 0
    for n in sizes:
        r = n % 8
        tails = 5 * (n // 8) + 2 * (r // 3) + r % 3
        out.append((first, n, off, 2 * n + tails))
        first, off = first + n, off + 2 * n + tails
    return out, off


SUBSETS, SLOTS = _subsets((8, 8, 3, 1))
MAXSUB = max(s[1] for s in SUBSETS)


def _split(v):
    one = v.astype(BF16)
    rest = v - one.astype(F32)
    two = rest.astype(BF16)
    return one, two, (rest - two.astype(F32)).astype(BF16)


def _dot(p, q):
    return jnp.dot(p, q, preferred_element_type=F32)


def _dot_nt(p, q):
    return lax.dot_general(p, q, NT, preferred_element_type=F32)


def _padq(v):
    return jnp.pad(v, ((0, 0), (0, QP - QL)))


def kernel(b_hbm, ct_hbm, met_hbm, out_ref,
           b_ref, ct_ref, met_ref, c_ref, ctt, dm_ref, s_ref, snd, rcv, hl, m_ref, mx, mr, t_ref, w_ref,
           ga_acc, ga_ref, gr_ref, j_ref, jown, jsend, jrecv, kacc, xacc, ksend, krecv,
           bsem, isem, hs_sem, hr_sem, ms_sem, mr_sem, gs_sem, gr_sem, js_sem, jr_sem, ks_sem, kr_sem):
    a = lax.axis_index('aux')
    o = lax.axis_index('orb')
    x, c = o // 2, o % 2
    sys = lax.axis_index('sys')

    def peer(k):
        return (a + k // 4) % 2, (x + (k // 2) % 2) % 2, (c + k % 2) % 2

    def device(k):
        pa, px, pc = peer(k)
        return (sys, pa, px * 2 + pc)

    def remote(src, dst, ssem, rsem, k):
        return pltpu.make_async_remote_copy(src_ref=src, dst_ref=dst, send_sem=ssem, recv_sem=rsem,
                                            device_id=device(k), device_id_type=MESH)

    def b_copy(j):
        first, n = ((0, 8), (8, 8), (16, 16), (32, 16))[j]
        return pltpu.make_async_copy(b_hbm.at[pl.ds(first, n)], b_ref.at[pl.ds(first, n)], bsem.at[j])

    def all_sent(ref, sem):
        remote(ref, ref, sem, sem, 0).wait_send()

    def all_here(ref, sem):
        remote(ref, ref, sem, sem, 0).wait_recv()

    def h_copy(k, g, s):
        _, _, off, n = SUBSETS[s]
        return remote(snd.at[k - 1, g, pl.ds(off, n)], rcv.at[k, g, pl.ds(off, n)],
                      hs_sem, hr_sem.at[g, s], k)

    FAR, NEAR = (4, 6, 5, 7), (2, 3, 1)

    def h_send(g, s, ks=(4, 6, 2, 5, 7, 3, 1)):
        for k in ks:
            h_copy(k, g, s).start()

    def m_copy(step):
        mine = o if step < 3 else (1 - x) * 2 + c
        src = mx.at[pl.ds(pl.multiple_of(o * MQ - (o // 3) * (4 * MQ - QL), 8), MQ)] if step == 0 else mr.at[mine]
        return remote(src, mr.at[mine], ms_sem, mr_sem.at[min(step, 2)], (4, 2, 1, 1)[step])

    def g_copy(k):
        return remote(ga_ref, gr_ref.at[k], gs_sem, gr_sem, k)

    def j_copy():
        return remote(jsend, jrecv, js_sem, jr_sem, 4)

    def k_copy(k):
        return remote(ksend.at[k], krecv.at[k], ks_sem, kr_sem, k)

    ct_copy = pltpu.make_async_copy(ct_hbm, ct_ref, isem.at[0])
    met_copy = pltpu.make_async_copy(met_hbm, met_ref, isem.at[1])
    ct_copy.start()
    met_copy.start()
    for j in range(2):
        b_copy(j).start()

    barrier = pltpu.get_barrier_semaphore()
    for k in range(1, 8):
        pl.semaphore_signal(barrier, inc=1, device_id=device(k), device_id_type=MESH)

    ct_copy.wait()
    for j, term in enumerate(_split(ct_ref[...])):
        c_ref[j] = term

    met_copy.wait()
    met = met_ref[...]
    low, high = _padq(met[:, :QL]), _padq(met[:, QL:])
    own = jnp.where(a == 0, low, high)
    mx[...] = own
    with jax.named_scope('barrier'):
        pl.semaphore_wait(barrier, 7)

    def m_store(block, row, col):
        for j, term in enumerate(_split(block)):
            m_ref[pl.ds(j * 2 * QP + row, block.shape[0]), pl.ds(col, QP)] = term

    lane = lax.broadcasted_iota(jnp.int32, (GROUP, 128), 1)

    def density_rows():
        ctt[...] = ct_ref[...].T
        rows = ctt[pl.ds(pl.multiple_of(o * ROWS, 8), ROWS), :]
        col = lax.broadcasted_iota(jnp.int32, (ROWS, COLS), 1)
        masked = [jnp.where((col >= d * OCC) & (col < (d + 1) * OCC), rows, 0.0) for d in range(DENS)]
        dens = jnp.dot(jnp.concatenate(masked, axis=0), ct_ref[...], precision=HIGHEST, preferred_element_type=F32)
        dm_ref[...] = jnp.zeros_like(dm_ref)
        for d in range(DENS):
            dm_ref[:, d, :] = dens[d * ROWS:(d + 1) * ROWS]

    def half_transform(g, start, n, with_gamma):
        def body(p, ga):
            m = g * GROUP + 2 * p
            b1, b2, b3 = _split(jnp.concatenate([_padq(b_ref[m]), _padq(b_ref[m + 1])], axis=1))
            terms = [c_ref[j, pl.ds(start, n), :] for j in range(3)]
            if with_gamma:
                extra = _split(dm_ref[pl.ds(m, 2)].reshape(16, L))
                terms = [jnp.concatenate(pair, axis=0) for pair in zip(terms, extra)]
            w = terms[0].shape[0]
            lhs = jnp.concatenate(terms, axis=0)
            r1, r2, r3 = _dot(lhs, b1), _dot(lhs[:2 * w], b2), _dot(lhs[:w], b3)
            h = r1[:w] + ((r1[w:2 * w] + r2[:w]) + (r1[2 * w:] + (r2[w:] + r3)))
            for q in range(2):
                row = pl.multiple_of((2 * p + q) * STRIDE + start, 8)
                for t in range(3):
                    s_ref[t, pl.ds(row, n), :] = h[:n, q * QP + t * 128:q * QP + (t + 1) * 128]
            if with_gamma:
                ga = ga + h[n:n + 8, :QP] + h[n + 8:, QP:]
            return ga

        return body

    def run_half(g, start, n, with_gamma, waits):
        body = half_transform(g, start, n, with_gamma)
        ga = (jnp.zeros((8, QP), F32) if g == 0 else ga_acc[...]) if with_gamma else 0
        for j in range(2):
            if waits and (g == 0 or j == 0):
                b_copy(j if g == 0 else g + 1).wait()
                if g == 0 and j == 1:
                    b_copy(2).start()
                    b_copy(3).start()
            ga = lax.fori_loop(2 * j, 2 * j + 2, lambda p, v: body(2 * p + 1, body(2 * p, v)), ga)
        if with_gamma:
            ga_acc[...] = ga
            if g == GROUPS - 1:
                ga_ref[...] = ga[:DENS]

    def pack(k, g, dst):
        pa, px, pc = peer(k)
        first = (pa * 4 + px * 2 + pc) * MINE

        def load(t, i):
            return s_ref[t, pl.ds(first + i, GROUP, stride=STRIDE), :]

        for i0, n, off, _ in SUBSETS:
            for i in range(n):
                dst[off + i] = load(0, i0 + i).astype(BF16)
                dst[off + n + i] = load(1, i0 + i).astype(BF16)
            at, i = off + 2 * n, i0
            while i < i0 + n:
                if i0 + n - i >= 8:
                    v = [load(2, i + j) for j in range(8)]
                    roll = lambda j, by: pltpu.roll(v[j], by, 1)
                    free = [roll(5, 80), jnp.where(lane < 112, roll(5, 32), roll(7, 64)), roll(6, 80),
                            jnp.where(lane < 112, roll(6, 32), roll(7, 48)), roll(7, 80)]
                    i += 8
                elif i0 + n - i >= 3:
                    v = [load(2, i + j) for j in range(3)]
                    free = [pltpu.roll(v[2], 80, 1), pltpu.roll(v[2], 32, 1)]
                    i += 3
                else:
                    v, free = [load(2, i)], None
                    i += 1
                for j in range(len(free) if free else 1):
                    dst[at] = (jnp.where(lane < TAIL, v[j], free[j]) if free else v[j]).astype(BF16)
                    at += 1

    def pack_range(g, k0, k1):
        def body(k, carry):
            pack(k, g, snd.at[k - 1, g])
            return carry

        lax.fori_loop(k0, k1, body, 0)

    def pack_self(g):
        pack(0, g, rcv.at[0, g])
        first = (a * 4 + x * 2 + c) * MINE
        for i in range(MINE):
            for t in range(3):
                _, two, three = _split(s_ref[t, pl.ds(first + i, GROUP, stride=STRIDE), :])
                hl[0, g, i, :, pl.ds(t * 128, 128)] = two
                hl[1, g, i, :, pl.ds(t * 128, 128)] = three

    scope = jax.named_scope
    m_copy(0).start()
    with scope('far'):
        run_half(0, pl.multiple_of((1 - a) * HALFC, 16), HALFC, False, True)
    with scope('packfar'):
        pack_range(0, 4, 8)
    h_send(0, 0, FAR)
    with scope('dens'):
        density_rows()
    with scope('near'):
        run_half(0, pl.multiple_of(a * HALFC, 16), HALFC, True, False)
    with scope('packnear'):
        pack_range(0, 1, 4)
    h_send(0, 0, NEAR)
    h_send(0, 1, (4, 5))
    pack_self(0)
    with scope('half1'):
        run_half(1, 0, COLS, True, True)
    with scope('m0wait'):
        all_here(mr.at[o], mr_sem.at[0])
    m_copy(1).start()
    m_copy(2).start()
    h_send(0, 1, (6, 2, 7, 3, 1))
    with scope('pack1'):
        pack_range(1, 1, 8)
    pack_self(1)
    with scope('half2'):
        run_half(2, 0, COLS, True, True)
    for k in (4, 6, 2, 5, 7, 3, 1):
        g_copy(k).start()
    h_send(1, 0)
    with scope('pack2'):
        pack_range(2, 1, 8)
    h_send(2, 0)
    h_send(1, 1)
    h_send(2, 1)
    pack_self(2)
    with scope('m1wait'):
        all_here(mr.at[o], mr_sem.at[1])
    m_copy(3).start()

    met = met_ref[...]
    low, high = _padq(met[:, :QL]), _padq(met[:, QL:])
    own = jnp.where(a == 0, low, high)
    oth = jnp.where(a == 0, high, low)
    m_store(own, 0, 0)
    m_store(oth, 0, QP)
    m_store(jnp.pad(oth, ((0, QP - QL), (0, 0))).T, QP, 0)
    with jax.named_scope('m3wait'):
        all_here(mr.at[pl.ds(0, 2)], mr_sem.at[2])
    for q in range(3):
        m_store(mr[q], QP + q * MQ, QP)
    m_store(mr[3][4 * MQ - QL:], QP + 3 * MQ, QP)
    for j in range(3):
        m_ref[pl.ds(j * 2 * QP + QL, QP - QL), :] = jnp.zeros((QP - QL, 2 * QP), BF16)
        m_ref[pl.ds(j * 2 * QP + QP + QL, QP - QL), pl.ds(QP, QP)] = jnp.zeros((QP - QL, QP), BF16)

    def fit(s, g0, g1):
        i0, n, off, _ = SUBSETS[s]

        def half(k, g):
            first = rcv[k, g, pl.ds(off, n)].reshape(n * GROUP, 128)
            second = rcv[k, g, pl.ds(off + n, n)].reshape(n * GROUP, 128)
            at, tails, left = off + 2 * n, [], n
            roll = lambda v, by: pltpu.roll(v.astype(F32), by, 1)
            while left:
                if left >= 8:
                    v = [rcv[k, g, at + j] for j in range(5)]
                    late = [jnp.where(lane < 48, roll(v[0], 48), roll(v[1], 96)), jnp.where(lane < 48, roll(v[2], 48), roll(v[3], 96)),
                            jnp.where(lane < 48, roll(v[4], 48), jnp.where(lane < 64, roll(v[1], 64), roll(v[3], 80)))]
                    left -= 8
                elif left >= 3:
                    v = [rcv[k, g, at + j] for j in range(2)]
                    late = [jnp.where(lane < 48, roll(v[0], 48), roll(v[1], 96))]
                    left -= 3
                else:
                    v, late = [rcv[k, g, at]], []
                    left -= 1
                tails += v + [w.astype(BF16) for w in late]
                at += len(v)
            return jnp.concatenate([first, second, jnp.concatenate(tails, axis=0)], axis=1)

        def fit_group(g, carry):
            with jax.named_scope(f'hwait{s}'):
                all_here(rcv.at[pl.ds(1, 7), g, pl.ds(off, SUBSETS[s][3])], hr_sem.at[g, s])
            lhs = jnp.concatenate([jnp.concatenate([half(k, g), half(k + 4, g)], axis=1) for k in range(4)], axis=0)
            t = _dot(jnp.concatenate([lhs, lhs, lhs], axis=1), m_ref[...])
            h2 = hl[0, g, pl.ds(i0, n)].reshape(n * GROUP, QP)
            h3 = hl[1, g, pl.ds(i0, n)].reshape(n * GROUP, QP)
            ca = _dot(jnp.concatenate([h2, h3], axis=0), m_ref[pl.ds(0, QP), :])
            cb = _dot(h2, m_ref[pl.ds(2 * QP, QP), :])
            w = n * GROUP
            for k in range(4):
                _, px, pc = peer(k)
                part = t[k * w:(k + 1) * w]
                if k == 0:
                    part = part + (ca[:w] + (ca[w:] + cb))
                row = pl.multiple_of((px * 2 + pc) * ROWS + g * GROUP, GROUP)
                t_ref[pl.ds(0, n), pl.ds(row, GROUP), :] = part.reshape(n, GROUP, 2 * QP)
            return carry

        with jax.named_scope(f'fit{s}'):
            lax.fori_loop(g0, g1, fit_group, 0)

    def exchange_subset(s):
        n = SUBSETS[s][1]
        step = 4 if n % 4 == 0 else n

        def exchange(i, carry):
            terms = zip(*[_split(t_ref[step * i + j]) for j in range(step)])
            t1, t2, t3 = [jnp.concatenate(v, axis=1) for v in terms]
            both = _dot_nt(jnp.concatenate([t1, t2], axis=0), t2)
            kacc[...] += _dot_nt(t1, t1) + both[L:]
            xacc[...] += both[:L] + _dot_nt(t1, t3)
            return carry

        with jax.named_scope(f'exch{s}'):
            lax.fori_loop(0, n // step, exchange, 0)

    kacc[...] = jnp.zeros_like(kacc)
    xacc[...] = jnp.zeros_like(xacc)
    fit(0, 0, 1)

    with jax.named_scope('gwait'):
        all_here(gr_ref.at[pl.ds(1, 7)], gr_sem)
    for g in range(GROUPS):
        h_send(g, 2)
    gam = jnp.concatenate([ga_ref[...] + gr_ref[1] + gr_ref[2] + gr_ref[3],
                           gr_ref[4] + gr_ref[5] + gr_ref[6] + gr_ref[7]], axis=1)
    gam = jnp.concatenate([gam, jnp.zeros_like(gam)], axis=0)

    def stack(v):
        return jnp.concatenate([t.astype(F32) for t in _split(v)], axis=0).astype(BF16)

    def three(v, dot):
        r1, r2, r3 = dot(v, 0), dot(v[:16], 1), dot(v[:8], 2)
        return r1[:8] + ((r1[8:16] + r2[:8]) + (r1[16:] + (r2[8:] + r3)))

    fitted = three(stack(gam), lambda v, j: _dot(v, m_ref[pl.ds(j * 2 * QP, 2 * QP), :]))
    weights = three(stack(fitted), lambda v, j: _dot(v, m_ref[pl.ds(j * 2 * QP, 2 * QP), pl.ds(0, QP)]))
    wf = jnp.concatenate([t.astype(F32) for t in _split(weights)], axis=0)
    for q in range(4):
        blocks = [jnp.zeros((WPAD * q, QP), F32)] if q else []
        wide = jnp.concatenate(blocks + [wf, jnp.zeros((128 - 24 - WPAD * q, QP), F32)], axis=0)
        wt = wide.T.astype(BF16)
        for j in range(3):
            w_ref[pl.ds((3 * q + j) * QP, QP), :] = wt

    def coulomb(p, carry):
        terms = [t for q in range(4) for t in _split(_padq(b_ref[4 * p + q]))]
        r = _dot(jnp.concatenate(terms, axis=1), w_ref[...]).T
        for q in range(4):
            j_ref[4 * p + q] = r[WPAD * q:WPAD * q + 8] + (r[WPAD * q + 8:WPAD * q + 16] + r[WPAD * q + 16:WPAD * q + 24])
        return carry

    with jax.named_scope('coulomb'):
        lax.fori_loop(0, ROWS // 4, coulomb, 0)
    away = []
    for d in range(DENS):
        jd = j_ref[:, d, :]
        jown[d] = jnp.where(a == 0, jd[:, :96], jd[:, 96:])
        away.append(jnp.where(a == 0, jd[:, 96:], jd[:, :96]))
    jsend[...] = jnp.concatenate(away, axis=1)
    for g in range(GROUPS):
        h_send(g, 3)
    j_copy().start()


    fit(0, 1, GROUPS)
    exchange_subset(0)
    for s in range(1, len(SUBSETS)):
        fit(s, 0, GROUPS)
        exchange_subset(s)

    j_copy().wait_recv()
    theirs = jrecv[...]
    for d in range(DENS):
        jown[d] = 2.0 * (jown[d] + theirs[:, 96 * d:96 * (d + 1)])
    kacc[...] += xacc[...] + xacc[...].T
    for k in (7, 6, 5, 4, 3, 2, 1, 0):
        pa, px, pc = peer(k)
        rows = kacc[pl.ds(pl.multiple_of((px * 2 + pc) * ROWS, 8), ROWS), :]
        part = jnp.where(pa == 0, rows[:, :96], rows[:, 96:])
        if k:
            ksend[k] = part
        else:
            krecv[0] = part
    for k in (7, 6, 5, 4, 3, 2, 1):
        k_copy(k).start()
    with jax.named_scope('kwait'):
        all_here(krecv.at[pl.ds(1, 7)], kr_sem)
    for k in (0, 2, 4, 6):
        pa, px, _ = peer(k)
        d = pa * 2 + px
        out_ref[d] = jown[d] - (krecv[k] + krecv[k + 1])

    all_sent(snd, hs_sem)
    all_sent(gr_ref.at[pl.ds(1, 7)], gs_sem)
    all_sent(ksend.at[pl.ds(1, 7)], ks_sem)
    all_sent(mr, ms_sem)
    j_copy().wait_send()


def solution(mesh):
    def local_fock(ints_blk, metric_blk, orbitals):
        bt = jnp.transpose(ints_blk, (1, 2, 0))
        ct = jnp.transpose(orbitals, (0, 2, 1)).reshape(COLS, L)
        ns = len(SUBSETS)
        dma = pltpu.SemaphoreType.DMA
        return pl.pallas_call(
            kernel,
            out_shape=jax.ShapeDtypeStruct((DENS, ROWS, 96), F32),
            in_specs=[pl.BlockSpec(memory_space=pltpu.HBM)] * 3,
            out_specs=pl.BlockSpec(memory_space=pltpu.VMEM),
            scratch_shapes=[
                pltpu.VMEM((ROWS, L, QL), F32),
                pltpu.VMEM((COLS, L), F32),
                pltpu.VMEM((QL, 2 * QL), F32),
                pltpu.VMEM((3, COLS, L), BF16),
                pltpu.VMEM((L, COLS), F32),
                pltpu.VMEM((ROWS, 8, L), F32),
                pltpu.VMEM((3, GROUP * STRIDE, 128), F32),
                pltpu.VMEM((7, GROUPS, SLOTS, GROUP, 128), BF16),
                pltpu.VMEM((8, GROUPS, SLOTS, GROUP, 128), BF16),
                pltpu.VMEM((2, GROUPS, MINE, GROUP, QP), BF16),
                pltpu.VMEM((6 * QP, 2 * QP), BF16),
                pltpu.VMEM((QL, QP), F32),
                pltpu.VMEM((4, MQ, QP), F32),
                pltpu.VMEM((MAXSUB, L, 2 * QP), F32),
                pltpu.VMEM((12 * QP, 128), BF16),
                pltpu.VMEM((8, QP), F32),
                pltpu.VMEM((DENS, QP), F32),
                pltpu.VMEM((8, DENS, QP), F32),
                pltpu.VMEM((ROWS, 8, L), F32),
                pltpu.VMEM((DENS, ROWS, 96), F32),
                pltpu.VMEM((ROWS, DENS * 96), F32),
                pltpu.VMEM((ROWS, DENS * 96), F32),
                pltpu.VMEM((L, L), F32),
                pltpu.VMEM((L, L), F32),
                pltpu.VMEM((8, ROWS, 96), F32),
                pltpu.VMEM((8, ROWS, 96), F32),
                dma((4,)), dma((2,)), dma, dma((GROUPS, ns)), dma, dma((3,)),
                dma, dma, dma, dma, dma, dma,
            ],
            compiler_params=pltpu.CompilerParams(collective_id=0, has_side_effects=True, vmem_limit_bytes=56_360_000),
            cost_estimate=pl.CostEstimate(flops=25_000_000_000, bytes_accessed=16_000_000, transcendentals=0),
        )(bt, ct, metric_blk)

    return jax.shard_map(local_fock, mesh=mesh, in_specs=(P(('sys', 'aux'), 'orb', None), P(('sys', 'aux'), None), P('sys', None, None)), out_specs=P('sys', 'orb', 'aux'), check_vma=False)
```

profile of v0, /device:TPU:0, one launch (start us, length us, event | category | flops | bytes accessed | tf_op | source)
XLA Modules:
  0.0 76.7 jit_solution(5313343672560005793)
XLA Ops:
  0.0 76.1 %shard_map.37 = f32[4,48,96]{2,1,0:T(8,128)S(1)} custom-call(f32[48,192,336]{2,1,0:T(8,128)} %bitcast.4, f32[160,192]{1,0:T(8,128)} %bitcast.5, f32[336,672]{1,0:T(8,128)} %met_hbm.1), custom_call_target="tpu_custom_call" | custom-call | flops 24999999488 | bytes 16000000 | tf_op jit(solution)/shard_map/pallas_call | solution.py:448
  76.1 0.6 copy.5
where the time goes:
time: 76.8 us; the launch traced here: 76.7 us
  Pallas kernels  76.1 us (99%)
    pallas_call x1, Pallas kernels, local_fock(): pl.pallas_call(kernel, out_shape=jax.ShapeDtypeStruct((DENS, ROWS, 96), F...  76.1 us

commit v1 on v0

--- a/solution.py
+++ b/solution.py
@@ -101,9 +101,9 @@
             h_copy(k, g, s).start()
 
     def m_copy(step):
-        mine = o if step < 3 else (1 - x) * 2 + c
-        src = mx.at[pl.ds(pl.multiple_of(o * MQ - (o // 3) * (4 * MQ - QL), 8), MQ)] if step == 0 else mr.at[mine]
-        return remote(src, mr.at[mine], ms_sem, mr_sem.at[min(step, 2)], (4, 2, 1, 1)[step])
+        mine = o if step != 3 else (1 - x) * 2 + c
+        src = mx.at[pl.ds(pl.multiple_of(o * MQ - (o // 3) * (4 * MQ - QL), 8), MQ)] if step in (0, 4) else mr.at[mine]
+        return remote(src, mr.at[mine], ms_sem, mr_sem.at[(0, 1, 2, 2, 1)[step]], (4, 2, 1, 1, 6)[step])
 
     def g_copy(k):
         return remote(ga_ref, gr_ref.at[k], gs_sem, gr_sem, k)
@@ -238,6 +238,7 @@
 
     scope = jax.named_scope
     m_copy(0).start()
+    pl.when(c == 1)(lambda: m_copy(4).start())
     with scope('far'):
         run_half(0, pl.multiple_of((1 - a) * HALFC, 16), HALFC, False, True)
     with scope('packfar'):
@@ -256,7 +257,7 @@
         run_half(1, 0, COLS, True, True)
     with scope('m0wait'):
         all_here(mr.at[o], mr_sem.at[0])
-    m_copy(1).start()
+    pl.when(c == 0)(lambda: m_copy(1).start())
     m_copy(2).start()
     h_send(0, 1, (6, 2, 7, 3, 1))
     with scope('pack1'):

time: 76.8 us -> 76.7 us (level)
  no operation moved by 1% of the time
where the time goes in v1:
time: 76.7 us; the launch traced here: 76.6 us
  Pallas kernels  76 us (99%)
    pallas_call x1, Pallas kernels, local_fock(): pl.pallas_call(kernel, out_shape=jax.ShapeDtypeStruct((DENS, ROWS, 96), F...  76 us

profile of v1, /device:TPU:0, one launch (start us, length us, event | category | flops | bytes accessed | tf_op | source)
XLA Modules:
  0.0 76.6 jit_solution(6603133108447349143)
XLA Ops:
  0.0 76.0 %shard_map.37 = f32[4,48,96]{2,1,0:T(8,128)S(1)} custom-call(f32[48,192,336]{2,1,0:T(8,128)} %bitcast.4, f32[160,192]{1,0:T(8,128)} %bitcast.5, f32[336,672]{1,0:T(8,128)} %met_hbm.1), custom_call_target="tpu_custom_call" | custom-call | flops 24999999488 | bytes 16000000 | tf_op jit(solution)/shard_map/pallas_call | solution.py:449
  76.0 0.6 copy.5
